TPU v7x, 32 devices: a whole 2x2x4 slice. The times are simulated.
32 devices in a mesh: dp: 16 (over z, y, x), member: 2 (over core).
Axes of the slice: x: 2, y: 2, z: 4, core: 2. Of those that a mesh axis runs over, the one named last changes fastest.
Arguments:
- inputs: bfloat16 [24576, 393], P(('dp', 'member')), may hold values from -256 to 256
- targets: bfloat16 [24576, 377], P(('dp', 'member')), may hold values from -6 to 6
- bootstrap: int32 [2, 24576], P('member', 'dp'), may hold values from 0 to 1535
- lower_weight: bfloat16 [2, 393, 1024], P('member'), may hold values from -0.3125 to 0.3125
- lower_shift: float32 [2, 1024], P('member'), may hold values from -3 to 3
- upper_weight: bfloat16 [2, 1024, 377], P('member'), may hold values from -0.1875 to 0.1875
- upper_shift: float32 [2, 377], P('member'), may hold values from -3 to 3
- log_var: float32 [2, 377], P('member'), may hold values from -1 to 1
Outputs:
- lower_grad: float32 [2, 1024, 393], P('member', 'dp')
- bias_grad: float32 [2, 1024], P('member', 'dp')
- upper_grad: float32 [2, 1024, 377], P('member', 'dp')
- offset_grad: float32 [2, 377], P('member')
- noise_grad: float32 [2, 377], P('member')
- member_loss: float32 [2], P('member')
Inputs may be any that keep to these rules, and one draw needn't show every extreme that they name: bootstrap[m, r] is an offset within the aligned block of 1536 rows that holds row r.
All inputs are finite; a program needn't handle non-finite values.
Results may differ from a plain program's by a relative error of at most 0.00076.
Values may be sent and summed in bfloat16 or wider, within the bound.
A program may use at most 64 MiB of HBM per device.

v0:
```python
import jax
import jax.numpy as jnp
from jax import lax
from jax.sharding import PartitionSpec as P

H = 1024


def member_pass(
    picked, goal_rows, lower_weight, lower_shift, upper_weight, upper_shift, log_var, row_count
):
    pre_act = jnp.dot(picked, lower_weight, preferred_element_type=jnp.float32) + lower_shift
    hidden = jax.nn.silu(pre_act).astype(jnp.bfloat16)
    pred_mean = jnp.dot(hidden, upper_weight, preferred_element_type=jnp.float32) + upper_shift
    residual = pred_mean - goal_rows.astype(jnp.float32)
    scaled_err = residual * jnp.exp(-log_var)
    member_loss = 0.5 * jnp.sum(residual * scaled_err + log_var) / row_count
    grad_mean = scaled_err / row_count
    offset_grad = jnp.sum(grad_mean, axis=0)
    noise_grad = 0.5 * jnp.sum(1.0 - residual * scaled_err, axis=0) / row_count
    grad_half = grad_mean.astype(jnp.bfloat16)
    grad_hidden = lax.dot_general(
        grad_half, upper_weight, (((1,), (1,)), ((), ())), preferred_element_type=jnp.float32
    )
    gate_sig = jax.nn.sigmoid(pre_act)
    grad_pre = grad_hidden * gate_sig * (1.0 + pre_act * (1.0 - gate_sig))
    bias_grad = jnp.sum(grad_pre, axis=0)
    pre_half = grad_pre.astype(jnp.bfloat16)
    return (hidden, grad_half, pre_half, bias_grad, offset_grad, noise_grad, member_loss)


def outer_rows(left, right):
    return lax.dot_general(
        left, right, (((0,), (0,)), ((), ())), preferred_element_type=jnp.float32
    )


def feature_stats(inputs):
    values = inputs.astype(jnp.float32)
    row_count = inputs.shape[0] * lax.axis_size("dp") * lax.axis_size("member")
    col_total = lax.psum(jnp.sum(values, axis=0), ("dp", "member"))
    feature_mean = col_total / row_count
    centered = values - feature_mean
    col_spread = lax.psum(jnp.sum(centered * centered, axis=0), ("dp", "member"))
    feature_var = col_spread / row_count
    return (feature_mean, 1.0 / jnp.sqrt(feature_var + 1e-06))


def per_device(
    inputs, targets, bootstrap, lower_weight, lower_shift, upper_weight, upper_shift, log_var
):
    feature_mean, feature_scale = feature_stats(inputs)
    own_rows = ((inputs.astype(jnp.float32) - feature_mean) * feature_scale).astype(jnp.bfloat16)
    row_block, goal_block = (
        lax.all_gather(own_rows, "member", axis=0, tiled=True),
        lax.all_gather(targets, "member", axis=0, tiled=True),
    )
    row_count = goal_block.shape[0]
    pick_row = bootstrap[0]
    picked = row_block[pick_row]
    passes = [
        (picked,)
        + member_pass(
            picked,
            goal_block[pick_row],
            lower_weight[0],
            lower_shift[0],
            upper_weight[0],
            upper_shift[0],
            log_var[0],
            row_count,
        )
    ]
    share = H // lax.axis_size("dp")
    lower_list, upper_list = ([], [])
    picked, hidden, grad_half, pre_half, bias_one, offset_one, noise_one, loss_one = passes[0]

    def upper_term(start, count, hidden=hidden, grad_half=grad_half):
        return outer_rows(hidden, grad_half)

    def lower_term(start, count, pre_half=pre_half, picked=picked):
        return outer_rows(pre_half, picked)

    upper_list.append(
        lax.psum_scatter(
            upper_term(jnp.int32(0), share * lax.axis_size("dp")),
            "dp",
            scatter_dimension=0,
            tiled=True,
        )
    )
    lower_list.append(
        lax.psum_scatter(
            lower_term(jnp.int32(0), share * lax.axis_size("dp")),
            "dp",
            scatter_dimension=0,
            tiled=True,
        )
    )
    lower_grad = jnp.stack(lower_list)
    upper_grad = jnp.stack(upper_list)
    bias_sum = jnp.stack([item[4] for item in passes])
    offset_sum = jnp.stack([item[5] for item in passes])
    noise_sum = jnp.stack([item[6] for item in passes])
    loss_sum = jnp.stack([item[7] for item in passes])
    bias_total, offset_grad, noise_grad, member_loss = lax.psum(
        (bias_sum, offset_sum, noise_sum, loss_sum), "dp"
    )
    bias_grad = lax.dynamic_slice_in_dim(bias_total, lax.axis_index("dp") * share, share, 1)
    return (lower_grad, bias_grad, upper_grad, offset_grad, noise_grad, member_loss)


def solution(mesh):
    return jax.shard_map(
        per_device,
        mesh=mesh,
        in_specs=(
            P(("dp", "member"), None),
            P(("dp", "member"), None),
            P("member", "dp"),
            P("member", None, None),
            P("member", None),
            P("member", None, None),
            P("member", None),
            P("member", None),
        ),
        out_specs=(
            P("member", "dp", None),
            P("member", "dp"),
            P("member", "dp", None),
            P("member", None),
            P("member", None),
            P("member"),
        ),
        check_vma=False,
    )
```

profile of v0, /device:TPU:0, one launch (start us, length us, event | category | flops | bytes accessed | tf_op | source)
XLA Modules:
  0.0 339.9 jit_solution(8934908891919403699)
XLA Ops:
  7.2 0.0 copy-start
  7.2 0.0 all-gather.5.cloned.1.call-start
  7.2 0.7 all-gather.5.cloned.1.call-update
  7.9 0.0 copy-start.3
  7.9 0.0 copy-start.2
  7.9 0.0 copy-start.4
  7.9 0.0 all-gather.3.cloned.1.call-start
  8.0 1.3 copy.15
  9.3 0.2 convert_reduce_fusion
  9.5 42.0 %psum.42 = f32[393]{0:T(512)S(1)} all-reduce(f32[393]{0:T(512)S(1)} %convert_reduce_fusion), channel_id=1, replica_groups=mesh['dp'=16,'member'=2] {'dp','member'}, use_global_device_ids=true, to_apply=%region_1.0 | all-reduce | flops 393 | bytes 3144 | tf_op jit(solution)/shard_map/psum | solution.py:41
  51.5 0.3 fusion.7
  51.8 40.1 %psum.43 = f32[393]{0:T(512)S(1)} all-reduce(f32[393]{0:T(512)S(1)} %fusion.7), channel_id=1, replica_groups=mesh['dp'=16,'member'=2] {'dp','member'}, use_global_device_ids=true, to_apply=%region_3.0 | all-reduce | flops 393 | bytes 3144 | tf_op jit(solution)/shard_map/psum | solution.py:44
  91.9 1.1 fusion.8
  93.0 0.0 all-gather.3.cloned.1.call-update
  93.0 0.0 reduce-scatter.5.cloned.1.call-start
  93.1 0.0 copy-done.3
  93.1 0.0 copy-done.2
  93.2 0.0 copy-done.4
  93.2 0.0 all-gather.5.cloned.1.call-done
  93.2 6.4 %gather_fusion.1 = bf16[1536,377]{1,0:T(8,128)(2,1)} fusion(bf16[1536,377]{1,0:T(8,128)(2,1)} %all-gather.5.cloned.1.call-done, s32[2048]{0:T(1024)S(1)} %pad_clamp_fusion), kind=kCustom, calls=%fused_computation.1 | custom fusion | bytes 2322432 | tf_op jit(solution)/shard_map/gather | solution.py:65
  99.7 0.0 copy-start.6
  99.7 3.9 %all-gather.3.cloned.1.call-done = bf16[1536,393]{1,0:T(8,128)(2,1)} async-done(((bf16[768,393]{1,0:T(8,128)(2,1)}), bf16[1536,393]{1,0:T(8,128)(2,1)}) %all-gather.3.cloned.1.call-update) | async-done | bytes 1207312 | tf_op jit(solution)/shard_map/all_gather | solution.py:55
  103.6 6.5 %gather_fusion = bf16[1536,393]{1,0:T(8,128)(2,1)S(1)} fusion(bf16[1536,393]{1,0:T(8,128)(2,1)} %all-gather.3.cloned.1.call-done, s32[2048]{0:T(1024)S(1)} %pad_clamp_fusion), kind=kCustom, calls=%fused_computation | custom fusion | bytes 2420736 | tf_op jit(solution)/shard_map/gather | solution.py:60
  110.1 0.0 copy-done
  110.1 0.0 copy-done.6
  110.1 0.0 copy-start.1
  110.1 0.0 copy-start.5
  110.1 5.1 %multiply_convert_fusion = (bf16[1536,1024]{1,0:T(8,128)(2,1)S(1)}, f32[1536,1024]{1,0:T(8,128)}) fusion(f32[1024]{0:T(1024)S(1)} %bitcast.29, bf16[1536,393]{1,0:T(8,128)(2,1)S(1)} %gather_fusion, bf16[1,393,1024]{2,1,0:T(8,128)(2,1)S(1)} %copy-done), kind=kOutput, calls=%fused_computation.3 | convolution fusion | flops 1245708288 | bytes 11453440 | tf_op jit(solution)/shard_map/dot_general | solution.py:12
  115.2 0.0 copy-done.1
  115.2 0.0 copy-done.5
  115.2 3.2 add_reduce_fusion
  118.4 0.0 copy-start.7
  118.4 1.4 copy-done.7
  119.8 3.0 fusion.13
  122.8 0.0 reduce-scatter.5.cloned.1.call-update
  122.9 0.2 reduce-scatter.3.cloned.1.call-start
  123.1 6.4 %fusion.20 = (f32[1024]{0:T(1024)S(1)}, bf16[1536,1024]{1,0:T(8,128)(2,1)S(1)}) fusion(f32[1536,1024]{1,0:T(8,128)} %get-tuple-element.16, f32[1024]{0:T(1024)S(1)} %bitcast.30, bf16[1,1024,377]{2,1,0:T(8,128)(2,1)S(1)} %copy-done.5, f32[1536,377]{1,0:T(8,128)} %copy-done.7, f32[377]{0:T(512)S(1)} %get-tuple-element.10), kind=kOutput, calls=%fused_computation.37 | convolution fusion | flops 1204977152 | bytes 12535268 | tf_op jit(solution)/shard_map/dot_general | solution.py:22
  129.5 3.2 fusion
  132.7 0.0 reduce-scatter.3.cloned.1.call-update
  133.4 43.6 %all-reduce = (f32[1,1024]{1,0:T(1,128)S(1)}, f32[1,377]{1,0:T(1,128)}, f32[1,377]{1,0:T(1,128)}, f32[1]{0:T(128)}) all-reduce(f32[1,1024]{1,0:T(1,128)S(1)} %bitcast.26, f32[1,377]{1,0:T(1,128)S(1)} %stack.19, f32[1,377]{1,0:T(1,128)S(1)} %div.37, f32[1]{0:T(128)} %bitcast.7), channel_id=1, replica_groups=mesh['dp'=16,'member'=2] {'dp'}, use_global_device_ids=true, to_apply=%region_6.7 | all-reduce | flops 1779 | bytes 14232 | tf_op jit(solution)/shard_map/psum | solution.py:106
  177.0 0.6 constant_dynamic-slice_fusion
  177.6 72.6 %reduce-scatter.5.cloned.1.call-done = f32[64,377]{1,0:T(8,128)} async-done(((f32[1024,377]{1,0:T(8,128)}), f32[64,377]{1,0:T(8,128)}) %reduce-scatter.5.cloned.1.call-update) | async-done | bytes 96528 | tf_op jit(solution)/shard_map/reduce_scatter | solution.py:85
  250.3 83.1 %reduce-scatter.3.cloned.1.call-done = f32[64,393]{1,0:T(8,128)} async-done(((f32[1024,393]{1,0:T(8,128)}), f32[64,393]{1,0:T(8,128)}) %reduce-scatter.3.cloned.1.call-update) | async-done | bytes 100624 | tf_op jit(solution)/shard_map/reduce_scatter | solution.py:93
  (9 shorter events, 0.1 us)
Async XLA Ops:
  7.2 102.9 %copy-start = (bf16[1,393,1024]{2,1,0:T(8,128)(2,1)S(1)}, bf16[1,393,1024]{2,1,0:T(8,128)(2,1)}, u32[]{:S(2)}) copy-start(bf16[1,393,1024]{2,1,0:T(8,128)(2,1)} %param.11) | copy-start | bytes 2414596
  7.2 86.0 %all-gather.5.cloned.1.call-start = ((), (), s32[]{:S(2)}) async-start(), calls=%async_computation.3 | async-start | bytes 1769472 | tf_op jit(solution)/shard_map/all_gather | solution.py:56
  7.9 85.2 %copy-start.3 = (f32[1,377]{1,0:T(1,128)S(1)}, f32[1,377]{1,0:T(1,128)}, u32[]{:S(2)}) copy-start(f32[1,377]{1,0:T(1,128)} %param.14) | copy-start | bytes 4528
  7.9 85.2 %copy-start.2 = (s32[1,1536]{1,0:T(1,128)S(1)}, s32[1,1536]{1,0:T(1,128)}, u32[]{:S(2)}) copy-start(s32[1,1536]{1,0:T(1,128)} %param.10) | copy-start | bytes 18436
  7.9 85.2 %copy-start.4 = (f32[1,377]{1,0:T(1,128)S(1)}, f32[1,377]{1,0:T(1,128)}, u32[]{:S(2)}) copy-start(f32[1,377]{1,0:T(1,128)} %param.15) | copy-start | bytes 4528
  7.9 95.6 %all-gather.3.cloned.1.call-start = ((), (), s32[]{:S(2)}) async-start(), calls=%async_computation.2 | async-start | bytes 2359296 | tf_op jit(solution)/shard_map/all_gather | solution.py:55
  93.0 157.2 %reduce-scatter.5.cloned.1.call-start = ((), (), s32[]{:S(2)}) async-start(), calls=%async_computation.5 | async-start | bytes 1671168 | tf_op jit(solution)/shard_map/reduce_scatter | solution.py:85
  99.7 10.4 %copy-start.6 = (f32[1,1024]{1,0:T(1,128)S(1)}, f32[1,1024]{1,0:T(1,128)}, u32[]{:S(2)}) copy-start(f32[1,1024]{1,0:T(1,128)} %param.12) | copy-start | bytes 12292
  110.1 5.1 %copy-start.1 = (bf16[1536,377]{1,0:T(8,128)(2,1)S(1)}, bf16[1536,377]{1,0:T(8,128)(2,1)}, u32[]{:S(2)}) copy-start(bf16[1536,377]{1,0:T(8,128)(2,1)} %gather_fusion.1) | copy-start | bytes 3474436
  110.1 5.1 %copy-start.5 = (bf16[1,1024,377]{2,1,0:T(8,128)(2,1)S(1)}, bf16[1,1024,377]{2,1,0:T(8,128)(2,1)}, u32[]{:S(2)}) copy-start(bf16[1,1024,377]{2,1,0:T(8,128)(2,1)} %param.13) | copy-start | bytes 2316292
  118.4 1.4 copy-start.7
  122.9 210.5 %reduce-scatter.3.cloned.1.call-start = ((), (), s32[]{:S(2)}) async-start(), calls=%async_computation.4 | async-start | bytes 2228224 | tf_op jit(solution)/shard_map/reduce_scatter | solution.py:93
Sparse Core Ops, SparseCore 0:
  9.5 11.9 all-gather.4
  93.1 10.3 all-gather.2
  123.0 127.2 reduce-scatter.4
  253.0 80.3 reduce-scatter.2
where the time goes:
time: 340 us
  waiting for transfers between devices  160 us (47%)
  blocking collectives  126 us (37%)
  matrix products  20.9 us (6%)
  local copies, waits for them, and re-layouts  16.3 us (5%)
  between operations  14.6 us (4%)
    reduce_scatter x1, waiting for transfers between devices, per_device(): lax.psum_scatter(lower_term(jnp.int32(0), share * lax.axis_size('dp')), '...  83.1 us
    reduce_scatter x1, waiting for transfers between devices, per_device(): lax.psum_scatter(upper_term(jnp.int32(0), share * lax.axis_size('dp')), '...  72.6 us
    psum x1, blocking collectives, per_device(): lax.psum((bias_sum, offset_sum, noise_sum, loss_sum), 'dp')  43.6 us
    psum x1, blocking collectives, feature_stats(): col_total = lax.psum(jnp.sum(values, axis=0), ('dp', 'member'))  42 us
    psum x1, blocking collectives, feature_stats(): lax.psum(jnp.sum(centered * centered, axis=0), ('dp', 'member'))  40.1 us
  transfers between devices with their start and end apart: 4, of which 3 were waited for; matrix products, arithmetic and copies ran while one was open for 6% of the time, Pallas kernels for 0%

commit v1 on v0

--- a/solution.py
+++ b/solution.py
@@ -38,7 +38,7 @@
 def feature_stats(inputs):
     values = inputs.astype(jnp.float32)
     row_count = inputs.shape[0] * lax.axis_size("dp") * lax.axis_size("member")
-    col_total = lax.psum(jnp.sum(values, axis=0), ("dp", "member"))
+    col_total = lax.psum(lax.psum(jnp.sum(values, axis=0), "member"), "dp")
     feature_mean = col_total / row_count
     centered = values - feature_mean
     col_spread = lax.psum(jnp.sum(centered * centered, axis=0), ("dp", "member"))

time: 340 us -> 341 us (level)
    psum x1 -> x2, blocking collectives: 42 us -> 46 us  [feature_stats(): col_total = lax.psum(lax.psum(jnp.sum(values, axis=0), 'member'), 'dp')]
where the time goes in v1:
time: 341 us; the launch traced here: 340 us
  waiting for transfers between devices  160 us (47%)
  blocking collectives  126 us (37%)
  matrix products  20.9 us (6%)
  local copies, waits for them, and re-layouts  16.3 us (5%)
  between operations  14.6 us (4%)
    reduce_scatter x1, waiting for transfers between devices, per_device(): lax.psum_scatter(lower_term(jnp.int32(0), share * lax.axis_size('dp')), '...  83.3 us
    reduce_scatter x1, waiting for transfers between devices, per_device(): lax.psum_scatter(upper_term(jnp.int32(0), share * lax.axis_size('dp')), '...  72.5 us
    psum x2, blocking collectives, feature_stats(): col_total = lax.psum(lax.psum(jnp.sum(values, axis=0), 'member'), 'dp')  46 us
    psum x1, blocking collectives, per_device(): lax.psum((bias_sum, offset_sum, noise_sum, loss_sum), 'dp')  43.7 us
    psum x1, blocking collectives, feature_stats(): lax.psum(jnp.sum(centered * centered, axis=0), ('dp', 'member'))  36.9 us
  transfers between devices with their start and end apart: 4, of which 3 were waited for; matrix products, arithmetic and copies ran while one was open for 6% of the time, Pallas kernels for 0%

profile of v1, /device:TPU:0, one launch (start us, length us, event | category | flops | bytes accessed | tf_op | source)
XLA Modules:
  0.0 340.5 jit_solution(1131835604942940178)
XLA Ops:
  7.2 0.0 copy-start
  7.2 0.0 all-gather.5.cloned.1.call-start
  7.2 0.7 all-gather.5.cloned.1.call-update
  7.9 0.0 copy-start.3
  7.9 0.0 copy-start.2
  7.9 0.0 copy-start.4
  7.9 0.0 all-gather.3.cloned.1.call-start
  8.0 1.3 copy.15
  9.3 0.2 convert_reduce_fusion
  9.5 2.6 psum.49
  12.1 43.3 %psum.50 = f32[393]{0:T(512)S(1)} all-reduce(f32[393]{0:T(512)S(1)} %psum.49), channel_id=1, replica_groups=mesh['dp'=16,'member'=2] {'dp'}, use_global_device_ids=true, to_apply=%region_2.0 | all-reduce | flops 393 | bytes 3144 | tf_op jit(solution)/shard_map/psum | solution.py:41
  55.5 0.3 fusion.7
  55.7 36.9 %psum.51 = f32[393]{0:T(512)S(1)} all-reduce(f32[393]{0:T(512)S(1)} %fusion.7), channel_id=1, replica_groups=mesh['dp'=16,'member'=2] {'dp','member'}, use_global_device_ids=true, to_apply=%region_4.0 | all-reduce | flops 393 | bytes 3144 | tf_op jit(solution)/shard_map/psum | solution.py:44
  92.6 1.1 fusion.8
  93.7 0.0 all-gather.3.cloned.1.call-update
  93.7 0.0 reduce-scatter.5.cloned.1.call-start
  93.8 0.0 copy-done.3
  93.8 0.0 copy-done.2
  93.8 0.0 copy-done.4
  93.9 0.0 all-gather.5.cloned.1.call-done
  93.9 6.4 %gather_fusion.1 = bf16[1536,377]{1,0:T(8,128)(2,1)} fusion(bf16[1536,377]{1,0:T(8,128)(2,1)} %all-gather.5.cloned.1.call-done, s32[2048]{0:T(1024)S(1)} %pad_clamp_fusion), kind=kCustom, calls=%fused_computation.1 | custom fusion | bytes 2322432 | tf_op jit(solution)/shard_map/gather | solution.py:65
  100.4 0.0 copy-start.6
  100.4 3.7 %all-gather.3.cloned.1.call-done = bf16[1536,393]{1,0:T(8,128)(2,1)} async-done(((bf16[768,393]{1,0:T(8,128)(2,1)}), bf16[1536,393]{1,0:T(8,128)(2,1)}) %all-gather.3.cloned.1.call-update) | async-done | bytes 1207312 | tf_op jit(solution)/shard_map/all_gather | solution.py:55
  104.1 6.5 %gather_fusion = bf16[1536,393]{1,0:T(8,128)(2,1)S(1)} fusion(bf16[1536,393]{1,0:T(8,128)(2,1)} %all-gather.3.cloned.1.call-done, s32[2048]{0:T(1024)S(1)} %pad_clamp_fusion), kind=kCustom, calls=%fused_computation | custom fusion | bytes 2420736 | tf_op jit(solution)/shard_map/gather | solution.py:60
  110.6 0.0 copy-done
  110.6 0.0 copy-done.6
  110.6 0.0 copy-start.1
  110.6 0.0 copy-start.5
  110.6 5.0 %multiply_convert_fusion = (bf16[1536,1024]{1,0:T(8,128)(2,1)S(1)}, f32[1536,1024]{1,0:T(8,128)}) fusion(f32[1024]{0:T(1024)S(1)} %bitcast.29, bf16[1536,393]{1,0:T(8,128)(2,1)S(1)} %gather_fusion, bf16[1,393,1024]{2,1,0:T(8,128)(2,1)S(1)} %copy-done), kind=kOutput, calls=%fused_computation.3 | convolution fusion | flops 1245708288 | bytes 11453440 | tf_op jit(solution)/shard_map/dot_general | solution.py:12
  115.7 0.0 copy-done.1
  115.7 0.0 copy-done.5
  115.7 3.2 add_reduce_fusion
  118.9 0.0 copy-start.7
  118.9 1.4 copy-done.7
  120.3 3.0 fusion.13
  123.3 0.0 reduce-scatter.5.cloned.1.call-update
  123.4 0.2 reduce-scatter.3.cloned.1.call-start
  123.6 6.4 %fusion.20 = (f32[1024]{0:T(1024)S(1)}, bf16[1536,1024]{1,0:T(8,128)(2,1)S(1)}) fusion(f32[1536,1024]{1,0:T(8,128)} %get-tuple-element.16, f32[1024]{0:T(1024)S(1)} %bitcast.30, bf16[1,1024,377]{2,1,0:T(8,128)(2,1)S(1)} %copy-done.5, f32[1536,377]{1,0:T(8,128)} %copy-done.7, f32[377]{0:T(512)S(1)} %get-tuple-element.10), kind=kOutput, calls=%fused_computation.37 | convolution fusion | flops 1204977152 | bytes 12535268 | tf_op jit(solution)/shard_map/dot_general | solution.py:22
  130.0 3.2 fusion
  133.2 0.0 reduce-scatter.3.cloned.1.call-update
  133.9 43.7 %all-reduce = (f32[1,1024]{1,0:T(1,128)S(1)}, f32[1,377]{1,0:T(1,128)}, f32[1,377]{1,0:T(1,128)}, f32[1]{0:T(128)}) all-reduce(f32[1,1024]{1,0:T(1,128)S(1)} %bitcast.26, f32[1,377]{1,0:T(1,128)S(1)} %stack.19, f32[1,377]{1,0:T(1,128)S(1)} %div.37, f32[1]{0:T(128)} %bitcast.7), channel_id=1, replica_groups=mesh['dp'=16,'member'=2] {'dp'}, use_global_device_ids=true, to_apply=%region_7.8 | all-reduce | flops 1779 | bytes 14232 | tf_op jit(solution)/shard_map/psum | solution.py:106
  177.6 0.6 constant_dynamic-slice_fusion
  178.2 72.5 %reduce-scatter.5.cloned.1.call-done = f32[64,377]{1,0:T(8,128)} async-done(((f32[1024,377]{1,0:T(8,128)}), f32[64,377]{1,0:T(8,128)}) %reduce-scatter.5.cloned.1.call-update) | async-done | bytes 96528 | tf_op jit(solution)/shard_map/reduce_scatter | solution.py:85
  250.7 83.3 %reduce-scatter.3.cloned.1.call-done = f32[64,393]{1,0:T(8,128)} async-done(((f32[1024,393]{1,0:T(8,128)}), f32[64,393]{1,0:T(8,128)}) %reduce-scatter.3.cloned.1.call-update) | async-done | bytes 100624 | tf_op jit(solution)/shard_map/reduce_scatter | solution.py:93
  (9 shorter events, 0.1 us)
Async XLA Ops:
  7.2 103.4 %copy-start = (bf16[1,393,1024]{2,1,0:T(8,128)(2,1)S(1)}, bf16[1,393,1024]{2,1,0:T(8,128)(2,1)}, u32[]{:S(2)}) copy-start(bf16[1,393,1024]{2,1,0:T(8,128)(2,1)} %param.11) | copy-start | bytes 2414596
  7.2 86.7 %all-gather.5.cloned.1.call-start = ((), (), s32[]{:S(2)}) async-start(), calls=%async_computation.3 | async-start | bytes 1769472 | tf_op jit(solution)/shard_map/all_gather | solution.py:56
  7.9 85.8 %copy-start.3 = (f32[1,377]{1,0:T(1,128)S(1)}, f32[1,377]{1,0:T(1,128)}, u32[]{:S(2)}) copy-start(f32[1,377]{1,0:T(1,128)} %param.14) | copy-start | bytes 4528
  7.9 85.9 %copy-start.2 = (s32[1,1536]{1,0:T(1,128)S(1)}, s32[1,1536]{1,0:T(1,128)}, u32[]{:S(2)}) copy-start(s32[1,1536]{1,0:T(1,128)} %param.10) | copy-start | bytes 18436
  7.9 85.9 %copy-start.4 = (f32[1,377]{1,0:T(1,128)S(1)}, f32[1,377]{1,0:T(1,128)}, u32[]{:S(2)}) copy-start(f32[1,377]{1,0:T(1,128)} %param.15) | copy-start | bytes 4528
  7.9 96.1 %all-gather.3.cloned.1.call-start = ((), (), s32[]{:S(2)}) async-start(), calls=%async_computation.2 | async-start | bytes 2359296 | tf_op jit(solution)/shard_map/all_gather | solution.py:55
  93.7 157.0 %reduce-scatter.5.cloned.1.call-start = ((), (), s32[]{:S(2)}) async-start(), calls=%async_computation.5 | async-start | bytes 1671168 | tf_op jit(solution)/shard_map/reduce_scatter | solution.py:85
  100.4 10.2 %copy-start.6 = (f32[1,1024]{1,0:T(1,128)S(1)}, f32[1,1024]{1,0:T(1,128)}, u32[]{:S(2)}) copy-start(f32[1,1024]{1,0:T(1,128)} %param.12) | copy-start | bytes 12292
  110.6 5.1 %copy-start.1 = (bf16[1536,377]{1,0:T(8,128)(2,1)S(1)}, bf16[1536,377]{1,0:T(8,128)(2,1)}, u32[]{:S(2)}) copy-start(bf16[1536,377]{1,0:T(8,128)(2,1)} %gather_fusion.1) | copy-start | bytes 3474436
  110.6 5.1 %copy-start.5 = (bf16[1,1024,377]{2,1,0:T(8,128)(2,1)S(1)}, bf16[1,1024,377]{2,1,0:T(8,128)(2,1)}, u32[]{:S(2)}) copy-start(bf16[1,1024,377]{2,1,0:T(8,128)(2,1)} %param.13) | copy-start | bytes 2316292
  118.9 1.4 copy-start.7
  123.4 210.6 %reduce-scatter.3.cloned.1.call-start = ((), (), s32[]{:S(2)}) async-start(), calls=%async_computation.4 | async-start | bytes 2228224 | tf_op jit(solution)/shard_map/reduce_scatter | solution.py:93
Sparse Core Ops, SparseCore 0:
  9.5 11.9 all-gather.4
  93.8 10.2 all-gather.2
  123.5 127.1 reduce-scatter.4
  253.4 80.5 reduce-scatter.2
